TPU v7x, 32 devices: a whole 2x2x4 slice. The times are simulated.
32 devices in a mesh: prefix: 4 (over z), resp: 8 (over y, x, core).
Axes of the slice: x: 2, y: 2, z: 4, core: 2. Of those that a mesh axis runs over, the one named last changes fastest.
Arguments:
- prompt_kv: bfloat16 [2, 128, 512], P(None, 'prefix'), may hold values from -6 to 6
- response_queries: bfloat16 [64, 128, 1792], P(('prefix', 'resp')), may hold values from -300 to 300
- resp_kv: bfloat16 [64, 128, 512], P(('prefix', 'resp')), may hold values from -6 to 6
- readout: bfloat16 [64, 128, 1792], P(('prefix', 'resp')), may hold values from -3 to 3
- slot_response: int32 [64], P(('prefix', 'resp')), may hold values from 0 to 63, each once
- lengths: int32 [64], replicated, may hold values from 32 to 128
- pair_prompt: int32 [32], replicated, may hold values from 0 to 1
- ref_margin: float32 [32], replicated, may hold values from -60 to 60
Outputs:
- margins: float32 [32], replicated
- grad_q: bfloat16 [64, 128, 1792], P(('prefix', 'resp'))
- grad_resp_kv: bfloat16 [64, 128, 512], P(('prefix', 'resp'))
- grad_prompt_kv: bfloat16 [2, 128, 512], P(None, 'prefix')
Inputs may be any that keep to these rules, and one draw needn't show every extreme that they name: `slot_response`: each response appears in exactly one slot; response 2 k is the chosen and 2 k + 1 the rejected response of pair k.
All inputs are finite; a program needn't handle non-finite values.
Results may differ from a plain program's by a relative error of at most 0.015.
Values may be sent and summed in bfloat16 or wider, within the bound.
A program may use at most 64 MiB of HBM per device.

v0:
```python
import jax
import jax.numpy as jnp
from jax import lax
from jax.sharding import PartitionSpec as P

QUERY_HEADS = 14
KEY_VALUE_HEADS = 2
HEAD_SIZE = 128


margin_beta = 0.1
loss_scale = 256.0


def unpack(packed_rows):
    row_block = packed_rows.shape[0]
    head_width = packed_rows.shape[1] // 2
    key_rows = packed_rows[:, :head_width].reshape(row_block, KEY_VALUE_HEADS, HEAD_SIZE)
    value_rows = packed_rows[:, head_width:].reshape(row_block, KEY_VALUE_HEADS, HEAD_SIZE)
    return (key_rows, value_rows)


def forward_pieces(query_rows, prompt_packed, own_packed, causal):
    prompt_keys, prompt_values = unpack(prompt_packed)
    own_keys, own_values = unpack(own_packed)
    scale_factor = HEAD_SIZE ** (-0.5)
    prompt_scores = (
        jnp.einsum("tgjd,kgd->gjtk", query_rows, prompt_keys, preferred_element_type=jnp.float32)
        * scale_factor
    )
    own_scores = (
        jnp.einsum("tgjd,kgd->gjtk", query_rows, own_keys, preferred_element_type=jnp.float32)
        * scale_factor
    )
    own_scores = jnp.where(causal, own_scores, -jnp.inf)
    row_max = jnp.maximum(
        jnp.max(prompt_scores, -1, keepdims=True), jnp.max(own_scores, -1, keepdims=True)
    )
    prompt_exp = jnp.exp(prompt_scores - row_max)
    own_exp = jnp.exp(own_scores - row_max)
    total = jnp.sum(prompt_exp, -1, keepdims=True) + jnp.sum(own_exp, -1, keepdims=True)
    prefix_probabilities = (prompt_exp / total).astype(jnp.bfloat16)
    self_probabilities = (own_exp / total).astype(jnp.bfloat16)
    attended = jnp.einsum(
        "gjtk,kgd->tgjd", prefix_probabilities, prompt_values, preferred_element_type=jnp.float32
    )
    attended = attended + jnp.einsum(
        "gjtk,kgd->tgjd", self_probabilities, own_values, preferred_element_type=jnp.float32
    )
    return (
        prompt_keys,
        prompt_values,
        own_keys,
        own_values,
        prefix_probabilities,
        self_probabilities,
        attended,
    )


def on_device(
    prompt_kv, response_queries, resp_kv, readout, slot_response, lengths, pair_prompt, ref_margin
):
    prompts = prompt_kv.shape[0]
    slots, slot_capacity, query_width = response_queries.shape
    query_groups = QUERY_HEADS // KEY_VALUE_HEADS
    pairs = ref_margin.shape[0]
    scale_factor = HEAD_SIZE ** (-0.5)
    full_kv = lax.all_gather(prompt_kv, "prefix", axis=1, tiled=True)
    prefix_length = full_kv.shape[1]
    positions = jnp.arange(slot_capacity)
    causal = positions[None, :] <= positions[:, None]
    pair_ids = jnp.arange(pairs)
    prompt_ids = jnp.arange(prompts)
    contrib = jnp.zeros((pairs,), jnp.float32)
    saved = []
    for position_index in range(slots):
        response = slot_response[position_index]
        pair_index = response // 2
        sign = 1.0 - 2.0 * (response % 2).astype(jnp.float32)
        valid = (positions < lengths[response]).astype(jnp.float32)
        prompt_index = pair_prompt[pair_index]
        prompt_packed = lax.dynamic_index_in_dim(full_kv, prompt_index, 0, keepdims=False)
        query_rows = response_queries[position_index].reshape(
            slot_capacity, KEY_VALUE_HEADS, query_groups, HEAD_SIZE
        )
        output_rows = readout[position_index].reshape(
            slot_capacity, KEY_VALUE_HEADS, query_groups, HEAD_SIZE
        )
        pieces = forward_pieces(query_rows, prompt_packed, resp_kv[position_index], causal)
        token_logp = jnp.sum(pieces[-1] * output_rows.astype(jnp.float32), axis=(1, 2, 3)) * valid
        contrib = contrib + jnp.where(pair_ids == pair_index, sign * jnp.sum(token_logp), 0.0)
        saved.append((pair_index, sign, valid, prompt_index, query_rows, output_rows, pieces))
    pair_sums = lax.psum(contrib, ("prefix", "resp"))
    margins = margin_beta * (pair_sums - ref_margin)
    weights = -loss_scale * margin_beta * jax.nn.sigmoid(-margins)
    partial_value = jnp.zeros((prompts, prefix_length, full_kv.shape[2]), jnp.float32)
    grad_rows = []
    grad_own = []
    for pair_index, sign, valid, prompt_index, query_rows, output_rows, pieces in saved:
        (
            prompt_keys,
            prompt_values,
            own_keys,
            own_values,
            prefix_probabilities,
            self_probabilities,
            attended,
        ) = pieces
        coefficient = weights[pair_index] * sign
        output_gradient = (
            coefficient * output_rows.astype(jnp.float32) * valid[:, None, None, None]
        ).astype(jnp.bfloat16)
        prompt_dprobs = jnp.einsum(
            "tgjd,kgd->gjtk", output_gradient, prompt_values, preferred_element_type=jnp.float32
        )
        own_dprobs = jnp.einsum(
            "tgjd,kgd->gjtk", output_gradient, own_values, preferred_element_type=jnp.float32
        )
        delta = jnp.transpose(
            jnp.sum(output_gradient.astype(jnp.float32) * attended, -1), (1, 2, 0)
        )[..., None]
        prefix_score_gradient = (
            prefix_probabilities.astype(jnp.float32) * (prompt_dprobs - delta) * scale_factor
        ).astype(jnp.bfloat16)
        self_score_gradient = (
            self_probabilities.astype(jnp.float32) * (own_dprobs - delta) * scale_factor
        ).astype(jnp.bfloat16)
        grad_queries = jnp.einsum(
            "gjtk,kgd->tgjd", prefix_score_gradient, prompt_keys, preferred_element_type=jnp.float32
        )
        grad_queries = grad_queries + jnp.einsum(
            "gjtk,kgd->tgjd", self_score_gradient, own_keys, preferred_element_type=jnp.float32
        )
        prompt_grad = jnp.concatenate(
            [
                jnp.einsum(
                    "hybi,bhyu->ihu",
                    prefix_score_gradient,
                    query_rows,
                    preferred_element_type=jnp.float32,
                ).reshape(prefix_length, KEY_VALUE_HEADS * HEAD_SIZE),
                jnp.einsum(
                    "hybi,bhyu->ihu",
                    prefix_probabilities,
                    output_gradient,
                    preferred_element_type=jnp.float32,
                ).reshape(prefix_length, KEY_VALUE_HEADS * HEAD_SIZE),
            ],
            axis=-1,
        )
        own_grad = jnp.concatenate(
            [
                jnp.einsum(
                    "hybi,bhyu->ihu",
                    self_score_gradient,
                    query_rows,
                    preferred_element_type=jnp.float32,
                ).reshape(slot_capacity, KEY_VALUE_HEADS * HEAD_SIZE),
                jnp.einsum(
                    "hybi,bhyu->ihu",
                    self_probabilities,
                    output_gradient,
                    preferred_element_type=jnp.float32,
                ).reshape(slot_capacity, KEY_VALUE_HEADS * HEAD_SIZE),
            ],
            axis=-1,
        )
        selector = (prompt_ids == prompt_index)[:, None, None]
        partial_value = partial_value + jnp.where(selector, prompt_grad[None], 0.0)
        grad_rows.append(grad_queries.reshape(slot_capacity, query_width).astype(jnp.bfloat16))
        grad_own.append(own_grad.astype(jnp.bfloat16))
    owned = lax.psum_scatter(partial_value, "prefix", scatter_dimension=1, tiled=True)
    grad_prompt = lax.psum(owned, "resp").astype(jnp.bfloat16)
    return (margins, jnp.stack(grad_rows), jnp.stack(grad_own), grad_prompt)


def solution(mesh):
    in_specs = (
        P(None, "prefix", None),
        P(("prefix", "resp"), None, None),
        P(("prefix", "resp"), None, None),
        P(("prefix", "resp"), None, None),
        P(("prefix", "resp")),
        P(),
        P(),
        P(),
    )
    out_specs = (
        P(),
        P(("prefix", "resp"), None, None),
        P(("prefix", "resp"), None, None),
        P(None, "prefix", None),
    )
    return jax.shard_map(
        on_device, mesh=mesh, in_specs=in_specs, out_specs=out_specs, check_vma=False
    )
```

profile of v0, /device:TPU:0, one launch (start us, length us, event | category | flops | bytes accessed | tf_op | source)
XLA Modules:
  0.0 167.4 jit_solution(1739317058117866416)
XLA Ops:
  7.2 1.3 fusion.48
  18.3 1.9 %iota_compare_fusion.1 = (pred[2]{0:T(512)(128)(4,1)}, pred[2]{0:T(512)(128)(4,1)}) fusion(s32[]{:T(128)} %bitcast.23, s32[]{:T(128)} %bitcast.2), kind=kLoop, calls=%fused_computation.89 | loop fusion | flops 4 | bytes 12 | tf_op jit(solution)/shard_map/eq | solution.py:169
  22.8 1.2 compare_convert_fusion.1
  24.0 15.6 %all_gather.3 = bf16[2,128,512]{2,1,0:T(8,128)(2,1)S(1)} all-gather(bf16[2,32,512]{2,1,0:T(8,128)(2,1)S(1)} %copy-done.20), channel_id=1, replica_groups=mesh['prefix'=4,'resp'=8] {'prefix'}, dimensions={1}, use_global_device_ids=true | all-gather | bytes 327680 | tf_op jit(solution)/shard_map/all_gather | solution.py:69
  44.5 1.1 divide_convert_fusion.1
  47.0 0.8 copy-done.12
  47.8 1.5 slice_convert_fusion.1
  49.3 1.5 copy.68
  51.1 1.2 multiply_reduce_fusion.3
  52.3 1.2 fusion.36
  53.5 1.5 copy.79
  55.0 2.0 %convolution_bitcast_fusion.2 = f32[128,2,7,128]{0,3,2,1:T(8,128)} fusion(bf16[128,2,128,1]{0,2,3,1:T(8,128)(2,1)} %bitcast.294, bf16[2,7,128,128]{2,3,1,0:T(8,128)(2,1)S(1)} %get-tuple-element.33), kind=kOutput, calls=%fused_computation.2 | convolution fusion | flops 58720256 | bytes 1441792 | tf_op jit(solution)/shard_map/gjtk,kgd->tgjd/dot_general | solution.py:47
  57.6 2.6 %multiply_reduce_fusion.2 = (f32[128]{0:T(128)S(1)}, f32[128,2,7,128]{0,3,2,1:T(8,128)}) fusion(f32[128,2,7,128]{0,3,2,1:T(8,128)S(1)} %bitcast.278, f32[128,2,7,128]{0,3,2,1:T(8,128)} %convolution_bitcast_fusion.2, bf16[128,2,128,1]{0,2,3,1:T(8,128)(2,1)S(1)} %bitcast.284, bf16[2,7,128,128]{2,3,1,0:T(8,128)(2,1)} %get-tuple-element.32), kind=kOutput, calls=%fused_computation.57 | convolution fusion | flops 59408256 | bytes 3277312 | tf_op jit(solution)/shard_map/gjtk,kgd->tgjd/dot_general | solution.py:44
  60.2 1.2 fusion.37
  62.7 40.7 %psum.14 = f32[32]{0:T(128)S(1)} all-reduce(f32[32]{0:T(128)S(1)} %fusion.38), channel_id=1, replica_groups=mesh['prefix'=4,'resp'=8] {'prefix','resp'}, use_global_device_ids=true, to_apply=%region_12.13 | all-reduce | flops 32 | bytes 256 | tf_op jit(solution)/shard_map/psum | solution.py:94
  106.2 1.4 multiply_reduce_fusion.1
  109.3 1.4 multiply_reduce_fusion
  113.0 0.9 select_add_fusion
  114.0 1.0 copy-done.3
  115.0 0.9 fusion.29
  121.6 0.7 copy-done.8
  123.5 1.0 pad_maximum_fusion
  124.6 11.3 %reduce-scatter.2.cloned.1.call-done = f32[2,32,512]{2,1,0:T(8,128)} async-done(((f32[2,128,512]{2,1,0:T(8,128)}), f32[2,32,512]{2,1,0:T(8,128)}) %reduce-scatter.2.cloned.1.call-update) | async-done | bytes 131088 | tf_op jit(solution)/shard_map/reduce_scatter | solution.py:173
  135.9 24.7 %all-reduce.1 = bf16[2,32,512]{2,1,0:T(8,128)(2,1)} all-reduce(f32[2,32,512]{2,1,0:T(8,128)} %reduce-scatter.2.cloned.1.call-done), channel_id=1, replica_groups=mesh['prefix'=4,'resp'=8] {'resp'}, use_global_device_ids=true, to_apply=%region_16.17 | all-reduce | flops 32768 | bytes 196608 | tf_op jit(solution)/shard_map/psum | solution.py:174
  (112 shorter events, 20.0 us)
Async XLA Ops:
  7.2 128.7 %reduce-scatter.2.cloned.1.call-start = ((), (), s32[]{:S(2)}) async-start(), calls=%async_computation.1 | async-start | bytes 655360 | tf_op jit(solution)/shard_map/reduce_scatter | solution.py:173
  11.8 3.3 %copy-start.23 = (s32[32]{0:T(128)S(1)}, s32[32]{0:T(128)}, u32[]{:S(2)}) copy-start(s32[32]{0:T(128)} %param.14) | copy-start | bytes 388
  11.8 12.2 %copy-start.20 = (bf16[2,32,512]{2,1,0:T(8,128)(2,1)S(1)}, bf16[2,32,512]{2,1,0:T(8,128)(2,1)}, u32[]{:S(2)}) copy-start(bf16[2,32,512]{2,1,0:T(8,128)(2,1)} %param.8) | copy-start | bytes 196612
  41.0 1.0 copy-start.18
  41.2 4.7 %copy-start.14 = (bf16[128,256]{0,1:T(8,128)(2,1)}, bf16[128,256]{0,1:T(8,128)(2,1)S(1)}, u32[]{:S(2)}) copy-start(bf16[128,256]{0,1:T(8,128)(2,1)S(1)} %copy.59) | copy-start | bytes 196612
  41.2 1.6 copy-start.11
  41.4 2.1 %copy-start.16 = (bf16[128,256]{0,1:T(8,128)(2,1)}, bf16[128,256]{0,1:T(8,128)(2,1)S(1)}, u32[]{:S(2)}) copy-start(bf16[128,256]{0,1:T(8,128)(2,1)S(1)} %copy.70) | copy-start | bytes 196612
  45.6 9.4 %copy-start = (bf16[2,7,128,128]{2,3,1,0:T(8,128)(2,1)}, bf16[2,7,128,128]{2,3,1,0:T(8,128)(2,1)S(1)}, u32[]{:S(2)}) copy-start(bf16[2,7,128,128]{2,3,1,0:T(8,128)(2,1)S(1)} %get-tuple-element.33) | copy-start | bytes 1376260
  46.7 1.2 copy-start.12
  47.8 3.0 %copy-start.2 = (bf16[2,7,128,128]{2,3,1,0:T(8,128)(2,1)}, bf16[2,7,128,128]{2,3,1,0:T(8,128)(2,1)S(1)}, u32[]{:S(2)}) copy-start(bf16[2,7,128,128]{2,3,1,0:T(8,128)(2,1)S(1)} %get-tuple-element.31) | copy-start | bytes 1376260
  47.8 3.2 %copy-start.5 = (bf16[2,7,128,128]{2,3,1,0:T(8,128)(2,1)}, bf16[2,7,128,128]{2,3,1,0:T(8,128)(2,1)S(1)}, u32[]{:S(2)}) copy-start(bf16[2,7,128,128]{2,3,1,0:T(8,128)(2,1)S(1)} %get-tuple-element.30) | copy-start | bytes 1376260
  62.7 40.7 %copy-start.25 = (f32[32]{0:T(128)S(1)}, f32[32]{0:T(128)}, u32[]{:S(2)}) copy-start(f32[32]{0:T(128)} %param.15) | copy-start | bytes 388
  106.2 1.4 copy-start.6
  108.3 0.8 copy-start.7
  109.3 1.4 copy-start.4
  111.4 0.8 copy-start.9
  113.9 1.0 copy-start.3
  115.9 1.0 copy-start.1
  116.9 0.8 copy-start.13
  118.4 0.8 copy-start.19
  119.4 1.0 copy-start.10
  119.9 0.9 copy-start.17
  121.3 1.0 copy-start.8
  121.3 1.0 copy-start.15
  (4 other events, 2.6 us)
Sparse Core Ops, SparseCore 0:
  114.1 21.7 reduce-scatter.1
where the time goes:
time: 169 us; the launch traced here: 167 us
  blocking collectives  81 us (48%)
  between operations  28.7 us (17%)
  local copies, waits for them, and re-layouts  17.5 us (10%)
  other arithmetic  15.8 us (9%)
  matrix products  13 us (8%)
  waiting for transfers between devices  11.4 us (7%)
    psum x1, blocking collectives, on_device(): pair_sums = lax.psum(contrib, ('prefix', 'resp'))  40.7 us
    psum x1, blocking collectives, on_device(): grad_prompt = lax.psum(owned, 'resp').astype(jnp.bfloat16)  24.7 us
    all_gather x1, blocking collectives, on_device(): full_kv = lax.all_gather(prompt_kv, 'prefix', axis=1, tiled=True)  15.6 us
    reduce_scatter x1, waiting for transfers between devices, on_device(): lax.psum_scatter(partial_value, 'prefix', scatter_dimension=1, tiled=True)  11.3 us
    unnamed x58, local copies, waits for them, and re-layouts  9.16 us
    dot_general x2, matrix products, forward_pieces(): jnp.einsum('gjtk,kgd->tgjd', prefix_probabilities, prompt_values, preferr...  3.82 us
  transfers between devices with their start and end apart: 1, of which 1 were waited for; matrix products, arithmetic and copies ran while one was open for 4% of the time, Pallas kernels for 0%

commit v1 on v0

v1 whole, which is shorter than its diff:
```python
import functools

import jax
import jax.numpy as jnp
from jax import lax
from jax.experimental import pallas as pl
from jax.experimental.pallas import tpu as pltpu
from jax.sharding import PartitionSpec as P

QUERY_HEADS = 14
KEY_VALUE_HEADS = 2
HEAD_SIZE = 128
LANES = 128
ROWS = 16

margin_beta = 0.1
loss_scale = 256.0
MESH = pl.DeviceIdType.MESH
F32 = jnp.float32
BF16 = jnp.bfloat16


def dot_nt(a, b):
    return lax.dot_general(a, b, (((1,), (1,)), ((), ())), preferred_element_type=F32)


def dot_nn(a, b):
    return lax.dot_general(a, b, (((1,), (0,)), ((), ())), preferred_element_type=F32)


def kernel(
    np_, nr,
    prompt_hbm, q_hbm, kv_hbm, ro_hbm, slot_ref, len_ref, pp_ref, ppv_ref, rm_ref,
    margins_out, gq_out, gkv_out, gp_out,
    full, qv, kvv, rov, ds_s, p_s, gq_s, gkv_s, g_send, g_all, info_all, fin_all, lanes_s,
    in_sem, pk_ssem, pk_rsem, g_ssem, g_rsem, i_ssem, i_rsem, f_ssem, f_rsem,
):
    n = np_ * nr
    prompts, local, width = prompt_hbm.shape
    slots, tokens, _ = q_hbm.shape
    pairs = rm_ref.shape[1]
    pl_w = info_all.shape[2]
    groups = QUERY_HEADS // KEY_VALUE_HEADS
    col_tiles = width // LANES
    tiles = (local // ROWS) * col_tiles
    total_len = full.shape[1]
    scale = HEAD_SIZE ** (-0.5)
    p = lax.axis_index("prefix")
    r = lax.axis_index("resp")
    me = p * nr + r

    def at_offset(k):
        other = lax.rem(me + k, n)
        return other, other // nr, lax.rem(other, nr)

    own_rows = full.at[:, pl.ds(pl.multiple_of(p * local, local), local), :]
    loads = [
        pltpu.make_async_copy(prompt_hbm, own_rows, in_sem.at[0]),
        pltpu.make_async_copy(q_hbm, qv, in_sem.at[1]),
        pltpu.make_async_copy(kv_hbm, kvv, in_sem.at[2]),
        pltpu.make_async_copy(ro_hbm, rov, in_sem.at[3]),
    ]
    for c in loads:
        c.start()

    barrier = pltpu.get_barrier_semaphore()

    def greet(k, carry):
        _, op, orr = at_offset(k)
        pl.semaphore_signal(barrier, inc=1, device_id=(op, orr), device_id_type=MESH)
        return carry

    lax.fori_loop(1, n, greet, 0)

    lanes_s[...] = jnp.zeros_like(lanes_s)
    lanes_s[0:1, 0:pairs] = rm_ref[...]
    lanes_s[1:2, 0:pairs] = ppv_ref[...].astype(F32)
    info_all[me] = jnp.zeros((info_all.shape[1], pl_w), F32)

    loads[0].wait()
    pl.semaphore_wait(barrier, n - 1)

    def prompt_copy(owner, to):
        rows = full.at[:, pl.ds(pl.multiple_of(owner * local, local), local), :]
        return pltpu.make_async_remote_copy(
            src_ref=rows, dst_ref=rows, send_sem=pk_ssem.at[to], recv_sem=pk_rsem.at[owner],
            device_id=(to, r), device_id_type=MESH,
        )

    others = [lax.rem(p + k, np_) for k in range(1, np_)]
    for o in others:
        prompt_copy(p, o).start()
    for c in loads[1:]:
        c.wait()
    for o in others:
        prompt_copy(o, p).wait_recv()

    causal = (
        lax.broadcasted_iota(jnp.int32, (tokens, tokens), 0)
        <= lax.broadcasted_iota(jnp.int32, (tokens, tokens), 1)
    )
    lane_t = lax.broadcasted_iota(jnp.int32, (1, tokens), 1)
    lane_k = lax.broadcasted_iota(jnp.int32, (1, pl_w), 1)

    def one_slot(s, carry):
        response = slot_ref[s]
        pair = lax.shift_right_logical(response, 1)
        sign = 1.0 - 2.0 * lax.bitwise_and(response, 1).astype(F32)
        valid = (lane_t < len_ref[response]).astype(F32)
        a = pp_ref[pair]
        logp = jnp.zeros((1, tokens), F32)
        for g in range(KEY_VALUE_HEADS):
            kc = slice(g * HEAD_SIZE, (g + 1) * HEAD_SIZE)
            vc = slice((KEY_VALUE_HEADS + g) * HEAD_SIZE, (KEY_VALUE_HEADS + g + 1) * HEAD_SIZE)
            keys = jnp.concatenate([full[a, :, kc], kvv[s, :, kc]], axis=0)
            values = jnp.concatenate([full[a, :, vc], kvv[s, :, vc]], axis=0)
            for j in range(groups):
                h = g * groups + j
                hc = slice(h * HEAD_SIZE, (h + 1) * HEAD_SIZE)
                jc = slice(j * tokens, (j + 1) * tokens)
                sc = dot_nt(keys, qv[s, :, hc])
                dp = dot_nt(values, rov[s, :, hc])
                sp = sc[:total_len]
                so = jnp.where(causal, sc[total_len:], -jnp.inf)
                top = jnp.maximum(
                    jnp.max(sp, axis=0, keepdims=True), jnp.max(so, axis=0, keepdims=True)
                )
                sc = jnp.concatenate([sp, so], axis=0)
                e = jnp.exp((sc - top) * scale)
                inv = valid / jnp.sum(e, axis=0, keepdims=True)
                pb = (e * inv).astype(BF16)
                pf = pb.astype(F32)
                delta = jnp.sum(pf * dp, axis=0, keepdims=True)
                logp = logp + delta
                p_s[:, jc] = pb
                ds_s[:, jc] = (pf * (dp - delta)).astype(BF16)
            gqt = dot_nn(keys.T, ds_s[...])
            for j in range(groups):
                h = g * groups + j
                hc = slice(h * HEAD_SIZE, (h + 1) * HEAD_SIZE)
                gq_s[s, :, hc] = gqt[:, j * tokens:(j + 1) * tokens].T
            heads = range(g * groups, (g + 1) * groups)
            qs = jnp.concatenate([qv[s, :, h * HEAD_SIZE:(h + 1) * HEAD_SIZE] for h in heads], axis=0)
            rs = jnp.concatenate([rov[s, :, h * HEAD_SIZE:(h + 1) * HEAD_SIZE] for h in heads], axis=0)
            gk = dot_nn(ds_s[...], qs) * scale
            gv = dot_nn(p_s[...], rs)
            gkv_s[s, :, kc] = gk[total_len:]
            gkv_s[s, :, vc] = gv[total_len:]
            for o in range(np_):
                for i in range(local // ROWS):
                    rows = slice(o * local + i * ROWS, o * local + (i + 1) * ROWS)
                    at = o * tiles + i * col_tiles
                    g_send[at + g, s] = gk[rows].astype(BF16)
                    g_send[at + KEY_VALUE_HEADS + g, s] = gv[rows].astype(BF16)
        hot = jnp.where(lane_k == pair, sign, 0.0)
        info_all[me, pl.ds(s, 1), :] = hot
        info_all[me, pl.ds(slots + s, 1), :] = hot * jnp.sum(logp, axis=1, keepdims=True)
        return carry

    lax.fori_loop(0, slots, one_slot, 0)

    def info_copy(sender, other, op, orr):
        return pltpu.make_async_remote_copy(
            src_ref=info_all.at[sender], dst_ref=info_all.at[sender],
            send_sem=i_ssem.at[other], recv_sem=i_rsem.at[sender],
            device_id=(op, orr), device_id_type=MESH,
        )

    def tile_copy(sender, other, op, orr):
        return pltpu.make_async_remote_copy(
            src_ref=g_send.at[op * tiles + orr], dst_ref=g_all.at[sender],
            send_sem=g_ssem.at[other], recv_sem=g_rsem.at[sender],
            device_id=(op, orr), device_id_type=MESH,
        )

    def when_owner(rank, f):
        if nr == tiles:
            f()
        else:
            pl.when(rank < tiles)(f)

    def send(k, carry):
        other, op, orr = at_offset(k)
        info_copy(me, other, op, orr).start()
        when_owner(orr, lambda: tile_copy(me, other, op, orr).start())
        return carry

    lax.fori_loop(1, n, send, 0)

    def take_own():
        g_all[me] = g_send[p * tiles + r]

    when_owner(r, take_own)

    def info_wait(k, carry):
        other, op, orr = at_offset(k)
        info_copy(other, other, op, orr).wait_recv()
        return carry

    lax.fori_loop(1, n, info_wait, 0)

    chunk = min(n, 32)

    def add_info(c, acc):
        return acc + jnp.sum(info_all[pl.ds(c * chunk, chunk)], axis=0)

    sums = lax.fori_loop(0, n // chunk, add_info, jnp.zeros((info_all.shape[1], pl_w), F32))
    pair_sums = jnp.sum(sums[slots:2 * slots], axis=0, keepdims=True)
    margins = margin_beta * (pair_sums - lanes_s[0:1, :])
    margins_out[...] = margins[:, 0:pairs]
    weights = -loss_scale * margin_beta * jax.nn.sigmoid(-margins)
    weights = jnp.where(lane_k < pairs, weights, 0.0)

    def finish_tile():
        def tile_wait(k, carry):
            other, op, orr = at_offset(k)
            pltpu.make_async_remote_copy(
                src_ref=g_send.at[0], dst_ref=g_all.at[other],
                send_sem=g_ssem.at[other], recv_sem=g_rsem.at[other],
                device_id=(op, orr), device_id_type=MESH,
            ).wait_recv()
            return carry

        lax.fori_loop(1, n, tile_wait, 0)

        def add_tiles(c, acc):
            x = info_all[pl.ds(c * chunk, chunk)]
            acc = list(acc)
            for a in range(prompts):
                wa = jnp.where(lanes_s[1:2, :] == float(a), weights, 0.0)
                ca = jnp.sum(x * wa[None], axis=-1, keepdims=True)
                for d in range(chunk):
                    for s in range(slots):
                        acc[a] = acc[a] + ca[d, s:s + 1, :] * g_all[c * chunk + d, s].astype(F32)
            return tuple(acc)

        zero = tuple(jnp.zeros((ROWS, LANES), F32) for _ in range(prompts))
        acc = lax.fori_loop(0, n // chunk, add_tiles, zero)
        for a in range(prompts):
            fin_all[r, a] = acc[a].astype(BF16)

        def fin_send(k, carry):
            orr = lax.rem(r + k, nr)
            pltpu.make_async_remote_copy(
                src_ref=fin_all.at[r], dst_ref=fin_all.at[r],
                send_sem=f_ssem.at[orr], recv_sem=f_rsem.at[r],
                device_id=(p, orr), device_id_type=MESH,
            ).start()
            return carry

        lax.fori_loop(1, nr, fin_send, 0)

    when_owner(r, finish_tile)

    for s in range(slots):
        coef = jnp.sum(info_all[me, s:s + 1, :] * weights, axis=1, keepdims=True)
        gq_out[s] = (gq_s[s] * (coef * scale)).astype(BF16)
        gkv_out[s] = (gkv_s[s] * coef).astype(BF16)

    def fin_copy(sender, other):
        return pltpu.make_async_remote_copy(
            src_ref=fin_all.at[sender], dst_ref=fin_all.at[sender],
            send_sem=f_ssem.at[other], recv_sem=f_rsem.at[sender],
            device_id=(p, other), device_id_type=MESH,
        )

    def fin_wait(k, carry):
        other = lax.rem(r + k, nr)
        when_owner(other, lambda: fin_copy(other, other).wait_recv())
        return carry

    lax.fori_loop(1, nr, fin_wait, 0)
    for t in range(tiles):
        i, j = divmod(t, col_tiles)
        for a in range(prompts):
            gp_out[a, i * ROWS:(i + 1) * ROWS, j * LANES:(j + 1) * LANES] = fin_all[t, a]

    def drain(k, carry):
        other, op, orr = at_offset(k)
        info_copy(me, other, op, orr).wait_send()
        when_owner(orr, lambda: tile_copy(me, other, op, orr).wait_send())
        return carry

    lax.fori_loop(1, n, drain, 0)
    for o in others:
        prompt_copy(p, o).wait_send()

    def drain_fin():
        def one(k, carry):
            fin_copy(r, lax.rem(r + k, nr)).wait_send()
            return carry

        lax.fori_loop(1, nr, one, 0)

    when_owner(r, drain_fin)


def on_device(np_, nr, prompt_kv, response_queries, resp_kv, readout, slot_response, lengths, pair_prompt, ref_margin):
    n = np_ * nr
    prompts, local, width = prompt_kv.shape
    slots, tokens, qw = response_queries.shape
    pairs = ref_margin.shape[0]
    pl_w = -(-pairs // LANES) * LANES
    total_len = local * np_
    groups = QUERY_HEADS // KEY_VALUE_HEADS
    tiles = (local // ROWS) * (width // LANES)
    assert nr >= tiles
    info_rows = -(-2 * slots // 8) * 8
    keys = total_len + tokens
    any_space = pl.BlockSpec(memory_space=pl.ANY)
    vmem = pl.BlockSpec(memory_space=pltpu.VMEM)
    smem = pl.BlockSpec(memory_space=pltpu.SMEM)
    dma = pltpu.SemaphoreType.DMA
    margins, gq, gkv, gp = pl.pallas_call(
        functools.partial(kernel, np_, nr),
        name="dpo_attention",
        out_shape=(
            jax.ShapeDtypeStruct((1, pairs), F32),
            jax.ShapeDtypeStruct(response_queries.shape, BF16),
            jax.ShapeDtypeStruct(resp_kv.shape, BF16),
            jax.ShapeDtypeStruct(prompt_kv.shape, BF16),
        ),
        in_specs=[any_space] * 4 + [smem] * 3 + [vmem] * 2,
        out_specs=(vmem,) * 4,
        scratch_shapes=[
            pltpu.VMEM((prompts, total_len, width), BF16),
            pltpu.VMEM((slots, tokens, qw), BF16),
            pltpu.VMEM((slots, tokens, width), BF16),
            pltpu.VMEM((slots, tokens, qw), BF16),
            pltpu.VMEM((keys, groups * tokens), BF16),
            pltpu.VMEM((keys, groups * tokens), BF16),
            pltpu.VMEM((slots, tokens, qw), F32),
            pltpu.VMEM((slots, tokens, width), F32),
            pltpu.VMEM((np_ * tiles, slots, ROWS, LANES), BF16),
            pltpu.VMEM((n, slots, ROWS, LANES), BF16),
            pltpu.VMEM((n, info_rows, pl_w), F32),
            pltpu.VMEM((tiles, prompts, ROWS, LANES), BF16),
            pltpu.VMEM((8, pl_w), F32),
            dma((4,)),
            dma((np_,)), dma((np_,)),
            dma((n,)), dma((n,)),
            dma((n,)), dma((n,)),
            dma((nr,)), dma((nr,)),
        ],
        compiler_params=pltpu.CompilerParams(collective_id=0, has_side_effects=True),
    )(
        prompt_kv, response_queries, resp_kv, readout, slot_response, lengths, pair_prompt,
        pair_prompt.reshape(1, pairs), ref_margin.reshape(1, pairs),
    )
    return margins.reshape(pairs), gq, gkv, gp


def solution(mesh):
    both = ("prefix", "resp")
    in_specs = (
        P(None, "prefix", None),
        P(both, None, None),
        P(both, None, None),
        P(both, None, None),
        P(both),
        P(),
        P(),
        P(),
    )
    out_specs = (
        P(),
        P(both, None, None),
        P(both, None, None),
        P(None, "prefix", None),
    )
    return jax.shard_map(
        functools.partial(on_device, mesh.shape["prefix"], mesh.shape["resp"]),
        mesh=mesh, in_specs=in_specs, out_specs=out_specs, check_vma=False,
    )
```

time: 169 us -> 40.1 us (0.24)
  blocking collectives: 81 us -> 0 us
  Pallas kernels: 0 us -> 34 us
  between operations: 28.7 us -> 0.65 us
  other arithmetic: 15.8 us -> 0 us
  matrix products: 13 us -> 0 us
  local copies, waits for them, and re-layouts: 17.5 us -> 4.84 us
  waiting for transfers between devices: 11.4 us -> 0 us
    psum x2 -> x0, blocking collectives: 65.4 us -> none  [the longest x1 40.7 us: on_device(): pair_sums = lax.psum(contrib, ('prefix', 'resp'))]
    pallas_call x0 -> x1, Pallas kernels: none -> 34 us  [on_device(): pl.pallas_call(functools.partial(kernel, np_, nr), name='dpo_attention',...]
    all_gather x1 -> x0, blocking collectives: 15.6 us -> none  [on_device(): full_kv = lax.all_gather(prompt_kv, 'prefix', axis=1, tiled=True)]
    dot_general x24 -> x0, matrix products: 13 us -> none  [the longest x2 3.82 us: forward_pieces(): jnp.einsum('gjtk,kgd->tgjd', prefix_probabilities, prompt_values, preferr...]
    reduce_scatter x1 -> x0, waiting for transfers between devices: 11.3 us -> none  [on_device(): lax.psum_scatter(partial_value, 'prefix', scatter_dimension=1, tiled=True)]
    reduce_sum x6 -> x0, other arithmetic: 5.93 us -> none  [the longest x2 2.81 us: on_device(): jnp.sum(output_gradient.astype(jnp.float32) * attended, -1)]
    convert_element_type x5 -> x0, other arithmetic: 4.7 us -> none  [the longest x2 1.8 us: on_device(): valid = (positions < lengths[response]).astype(jnp.float32)]
    unnamed x58 -> x10, local copies, waits for them, and re-layouts: 9.16 us -> 4.84 us
  transfers between devices with their start and end apart: 1 -> 0, of which waited for: 1 -> 0; matrix products, arithmetic and copies ran while one was open for 4% -> 0% of each run, Pallas kernels for 0% -> 0%
where the time goes in v1:
time: 40.1 us; the launch traced here: 39.5 us
  Pallas kernels  34 us (85%)
  local copies, waits for them, and re-layouts  4.84 us (12%)
  between operations  0.65 us (2%)
    pallas_call x1, Pallas kernels, on_device(): pl.pallas_call(functools.partial(kernel, np_, nr), name='dpo_attention',...  34 us
    unnamed x10, local copies, waits for them, and re-layouts  4.84 us

profile of v1, /device:TPU:0, one launch (start us, length us, event | category | flops | bytes accessed | tf_op | source)
XLA Modules:
  0.0 39.5 jit_solution(8598447178357441571)
XLA Ops:
  0.6 34.0 %dpo_attention.1 = (f32[1,32]{1,0:T(1,128)}, bf16[2,128,1792]{2,1,0:T(8,128)(2,1)}, bf16[2,128,512]{2,1,0:T(8,128)(2,1)}, bf16[2,32,512]{2,1,0:T(8,128)(2,1)}) custom-call(bf16[2,32,512]{2,1,0:T(8,128)(2,1)} %prompt_hbm.1, bf16[2,128,1792]{2,1,0:T(8,128)(2,1)} %q_hbm.1, bf16[2,128,512]{2,1,0:T(8,128)(2,1)} %kv_hbm.1, bf16[2,128,1792]{2,1,0:T(8,128)(2,1)} %ro_hbm.1, ...), custom_call_target="tpu_custom_call" | custom-call | tf_op jit(solution)/shard_map/dpo_attention/pallas_call | solution.py:314
  34.7 0.0 copy-start.2
  34.7 0.6 %copy-done.2 = f32[1,32]{1,0:T(1,128)S(1)} copy-done((f32[1,32]{1,0:T(1,128)S(1)}, f32[1,32]{1,0:T(1,128)}, u32[]{:S(2)}) %copy-start.2) | copy-done | bytes 152
  35.3 0.5 %copy.16 = f32[32]{0:T(128)} copy(f32[32]{0:T(128)S(1)} %bitcast.5) | data formatting | bytes 256
  35.8 0.0 copy-start
  35.8 2.2 %copy.17 = bf16[2,128,1792]{2,1,0:T(8,128)(2,1)} copy(bf16[2,128,1792]{2,1,0:T(8,128)(2,1)} %get-tuple-element.17) | data formatting | bytes 1835008
  38.0 0.0 copy-done
  38.0 0.0 copy-start.1
  38.0 0.7 %copy.18 = bf16[2,128,512]{2,1,0:T(8,128)(2,1)} copy(bf16[2,128,512]{2,1,0:T(8,128)(2,1)S(1)} %copy-done) | data formatting | bytes 524288
  38.7 0.2 copy-done.1
  38.9 0.6 %copy.19 = bf16[2,32,512]{2,1,0:T(8,128)(2,1)} copy(bf16[2,32,512]{2,1,0:T(8,128)(2,1)S(1)} %copy-done.1) | data formatting | bytes 131072
Async XLA Ops:
  34.7 0.6 %copy-start.2 = (f32[1,32]{1,0:T(1,128)S(1)}, f32[1,32]{1,0:T(1,128)}, u32[]{:S(2)}) copy-start(f32[1,32]{1,0:T(1,128)} %get-tuple-element.8) | copy-start | bytes 388
  35.8 2.2 %copy-start = (bf16[2,128,512]{2,1,0:T(8,128)(2,1)S(1)}, bf16[2,128,512]{2,1,0:T(8,128)(2,1)}, u32[]{:S(2)}) copy-start(bf16[2,128,512]{2,1,0:T(8,128)(2,1)} %get-tuple-element.18) | copy-start | bytes 786436
  38.0 0.9 %copy-start.1 = (bf16[2,32,512]{2,1,0:T(8,128)(2,1)S(1)}, bf16[2,32,512]{2,1,0:T(8,128)(2,1)}, u32[]{:S(2)}) copy-start(bf16[2,32,512]{2,1,0:T(8,128)(2,1)} %get-tuple-element.19) | copy-start | bytes 196612

commit v2 on v1

--- a/solution.py
+++ b/solution.py
@@ -31,9 +31,9 @@
 def kernel(
     np_, nr,
     prompt_hbm, q_hbm, kv_hbm, ro_hbm, slot_ref, len_ref, pp_ref, ppv_ref, rm_ref,
-    margins_out, gq_out, gkv_out, gp_out,
-    full, qv, kvv, rov, ds_s, p_s, gq_s, gkv_s, g_send, g_all, info_all, fin_all, lanes_s,
-    in_sem, pk_ssem, pk_rsem, g_ssem, g_rsem, i_ssem, i_rsem, f_ssem, f_rsem,
+    margins_out, gq_s, gkv_s, fin_out, coef_out,
+    full, qv, kvv, rov, ds_s, p_s, g_send, g_all, info_all, fin_all, lanes_s,
+    in_sem, pk_ssem, pk_rsem, pd_ssem, pd_rsem, g_ssem, g_rsem, i_ssem, i_rsem, f_ssem, f_rsem,
 ):
     n = np_ * nr
     prompts, local, width = prompt_hbm.shape
@@ -80,11 +80,26 @@
     loads[0].wait()
     pl.semaphore_wait(barrier, n - 1)
 
+    half = lax.rem(r, 2)
+    partner = r + 1 - 2 * half
+    half_width = width // 2
+
+    def half_of(owner, which):
+        rows = pl.ds(pl.multiple_of(owner * local, local), local)
+        return full.at[:, rows, pl.ds(pl.multiple_of(which * half_width, half_width), half_width)]
+
     def prompt_copy(owner, to):
-        rows = full.at[:, pl.ds(pl.multiple_of(owner * local, local), local), :]
+        part = half_of(owner, half)
         return pltpu.make_async_remote_copy(
-            src_ref=rows, dst_ref=rows, send_sem=pk_ssem.at[to], recv_sem=pk_rsem.at[owner],
+            src_ref=part, dst_ref=part, send_sem=pk_ssem.at[to], recv_sem=pk_rsem.at[owner],
             device_id=(to, r), device_id_type=MESH,
+        )
+
+    def pass_copy(owner, which):
+        part = half_of(owner, which)
+        return pltpu.make_async_remote_copy(
+            src_ref=part, dst_ref=part, send_sem=pd_ssem.at[owner], recv_sem=pd_rsem.at[owner],
+            device_id=(p, partner), device_id_type=MESH,
         )
 
     others = [lax.rem(p + k, np_) for k in range(1, np_)]
@@ -94,6 +109,9 @@
         c.wait()
     for o in others:
         prompt_copy(o, p).wait_recv()
+        pass_copy(o, half).start()
+    for o in others:
+        pass_copy(o, 1 - half).wait_recv()
 
     causal = (
         lax.broadcasted_iota(jnp.int32, (tokens, tokens), 0)
@@ -101,6 +119,26 @@
     )
     lane_t = lax.broadcasted_iota(jnp.int32, (1, tokens), 1)
     lane_k = lax.broadcasted_iota(jnp.int32, (1, pl_w), 1)
+
+    def info_copy(sender, other, op, orr):
+        return pltpu.make_async_remote_copy(
+            src_ref=info_all.at[sender], dst_ref=info_all.at[sender],
+            send_sem=i_ssem.at[other], recv_sem=i_rsem.at[sender],
+            device_id=(op, orr), device_id_type=MESH,
+        )
+
+    def tile_copy(s, sender, other, op, orr):
+        return pltpu.make_async_remote_copy(
+            src_ref=g_send.at[s, op * tiles + orr], dst_ref=g_all.at[sender, s],
+            send_sem=g_ssem.at[s, other], recv_sem=g_rsem.at[s, sender],
+            device_id=(op, orr), device_id_type=MESH,
+        )
+
+    def when_owner(rank, f):
+        if nr == tiles:
+            f()
+        else:
+            pl.when(rank < tiles)(f)
 
     def one_slot(s, carry):
         response = slot_ref[s]
@@ -150,45 +188,32 @@
                 for i in range(local // ROWS):
                     rows = slice(o * local + i * ROWS, o * local + (i + 1) * ROWS)
                     at = o * tiles + i * col_tiles
-                    g_send[at + g, s] = gk[rows].astype(BF16)
-                    g_send[at + KEY_VALUE_HEADS + g, s] = gv[rows].astype(BF16)
+                    g_send[s, at + g] = gk[rows].astype(BF16)
+                    g_send[s, at + KEY_VALUE_HEADS + g] = gv[rows].astype(BF16)
         hot = jnp.where(lane_k == pair, sign, 0.0)
         info_all[me, pl.ds(s, 1), :] = hot
         info_all[me, pl.ds(slots + s, 1), :] = hot * jnp.sum(logp, axis=1, keepdims=True)
+
+        def send_tile(k, c):
+            other, op, orr = at_offset(k)
+            when_owner(orr, lambda: tile_copy(s, me, other, op, orr).start())
+            return c
+
+        lax.fori_loop(1, n, send_tile, 0)
         return carry
 
     lax.fori_loop(0, slots, one_slot, 0)
-
-    def info_copy(sender, other, op, orr):
-        return pltpu.make_async_remote_copy(
-            src_ref=info_all.at[sender], dst_ref=info_all.at[sender],
-            send_sem=i_ssem.at[other], recv_sem=i_rsem.at[sender],
-            device_id=(op, orr), device_id_type=MESH,
-        )
-
-    def tile_copy(sender, other, op, orr):
-        return pltpu.make_async_remote_copy(
-            src_ref=g_send.at[op * tiles + orr], dst_ref=g_all.at[sender],
-            send_sem=g_ssem.at[other], recv_sem=g_rsem.at[sender],
-            device_id=(op, orr), device_id_type=MESH,
-        )
-
-    def when_owner(rank, f):
-        if nr == tiles:
-            f()
-        else:
-            pl.when(rank < tiles)(f)
 
     def send(k, carry):
         other, op, orr = at_offset(k)
         info_copy(me, other, op, orr).start()
-        when_owner(orr, lambda: tile_copy(me, other, op, orr).start())
         return carry
 
     lax.fori_loop(1, n, send, 0)
 
     def take_own():
-        g_all[me] = g_send[p * tiles + r]
+        for s in range(slots):
+            g_all[me, s] = g_send[s, p * tiles + r]
 
     when_owner(r, take_own)
 
@@ -210,15 +235,19 @@
     margins_out[...] = margins[:, 0:pairs]
     weights = -loss_scale * margin_beta * jax.nn.sigmoid(-margins)
     weights = jnp.where(lane_k < pairs, weights, 0.0)
+    for s in range(slots):
+        coef = jnp.sum(info_all[me, s:s + 1, :] * weights, axis=1, keepdims=True)
+        coef_out[s:s + 1, :] = jnp.broadcast_to(coef, (1, LANES))
 
     def finish_tile():
         def tile_wait(k, carry):
             other, op, orr = at_offset(k)
-            pltpu.make_async_remote_copy(
-                src_ref=g_send.at[0], dst_ref=g_all.at[other],
-                send_sem=g_ssem.at[other], recv_sem=g_rsem.at[other],
-                device_id=(op, orr), device_id_type=MESH,
-            ).wait_recv()
+            for s in range(slots):
+                pltpu.make_async_remote_copy(
+                    src_ref=g_send.at[s, 0], dst_ref=g_all.at[other, s],
+                    send_sem=g_ssem.at[s, other], recv_sem=g_rsem.at[s, other],
+                    device_id=(op, orr), device_id_type=MESH,
+                ).wait_recv()
             return carry
 
         lax.fori_loop(1, n, tile_wait, 0)
@@ -252,11 +281,6 @@
 
     when_owner(r, finish_tile)
 
-    for s in range(slots):
-        coef = jnp.sum(info_all[me, s:s + 1, :] * weights, axis=1, keepdims=True)
-        gq_out[s] = (gq_s[s] * (coef * scale)).astype(BF16)
-        gkv_out[s] = (gkv_s[s] * coef).astype(BF16)
-
     def fin_copy(sender, other):
         return pltpu.make_async_remote_copy(
             src_ref=fin_all.at[sender], dst_ref=fin_all.at[sender],
@@ -270,20 +294,19 @@
         return carry
 
     lax.fori_loop(1, nr, fin_wait, 0)
-    for t in range(tiles):
-        i, j = divmod(t, col_tiles)
-        for a in range(prompts):
-            gp_out[a, i * ROWS:(i + 1) * ROWS, j * LANES:(j + 1) * LANES] = fin_all[t, a]
+    fin_out[...] = fin_all[...]
 
     def drain(k, carry):
         other, op, orr = at_offset(k)
         info_copy(me, other, op, orr).wait_send()
-        when_owner(orr, lambda: tile_copy(me, other, op, orr).wait_send())
+        for s in range(slots):
+            when_owner(orr, lambda s=s: tile_copy(s, me, other, op, orr).wait_send())
         return carry
 
     lax.fori_loop(1, n, drain, 0)
     for o in others:
         prompt_copy(p, o).wait_send()
+        pass_copy(o, half).wait_send()
 
     def drain_fin():
         def one(k, carry):
@@ -293,6 +316,40 @@
         lax.fori_loop(1, nr, one, 0)
 
     when_owner(r, drain_fin)
+
+
+def finish(margins_ref, gq_ref, gkv_ref, fin_ref, coef_ref, margins_out, gq_out, gkv_out, gp_out, mv, qv, kvv, gpv, sems):
+    slots, tokens, qw = gq_ref.shape
+    tiles, prompts, _, _ = fin_ref.shape
+    width = gkv_ref.shape[2]
+    col_tiles = width // LANES
+    scale = HEAD_SIZE ** (-0.5)
+    pieces = 2
+    step = tokens // pieces
+    copies = []
+
+    def put(src, dst):
+        c = pltpu.make_async_copy(src, dst, sems.at[len(copies)])
+        c.start()
+        copies.append(c)
+
+    for s in range(slots):
+        coef = coef_ref[s:s + 1, 0:1]
+        for t in range(pieces):
+            rows = slice(t * step, (t + 1) * step)
+            qv[s, rows] = (gq_ref[s, rows] * (coef * scale)).astype(BF16)
+            put(qv.at[s, rows], gq_out.at[s, rows])
+        kvv[s] = (gkv_ref[s] * coef).astype(BF16)
+        put(kvv.at[s], gkv_out.at[s])
+    for t in range(tiles):
+        i, j = divmod(t, col_tiles)
+        for a in range(prompts):
+            gpv[a, i * ROWS:(i + 1) * ROWS, j * LANES:(j + 1) * LANES] = fin_ref[t, a]
+    put(gpv, gp_out)
+    mv[...] = margins_ref[...]
+    put(mv, margins_out)
+    for c in copies:
+        c.wait()
 
 
 def on_device(np_, nr, prompt_kv, response_queries, resp_kv, readout, slot_response, lengths, pair_prompt, ref_margin):
@@ -305,23 +362,25 @@
     groups = QUERY_HEADS // KEY_VALUE_HEADS
     tiles = (local // ROWS) * (width // LANES)
     assert nr >= tiles
-    info_rows = -(-2 * slots // 8) * 8
+    info_rows = 2 * slots
+    assert nr % 2 == 0
     keys = total_len + tokens
     any_space = pl.BlockSpec(memory_space=pl.ANY)
     vmem = pl.BlockSpec(memory_space=pltpu.VMEM)
     smem = pl.BlockSpec(memory_space=pltpu.SMEM)
     dma = pltpu.SemaphoreType.DMA
-    margins, gq, gkv, gp = pl.pallas_call(
+    partial_outs = pl.pallas_call(
         functools.partial(kernel, np_, nr),
         name="dpo_attention",
         out_shape=(
             jax.ShapeDtypeStruct((1, pairs), F32),
-            jax.ShapeDtypeStruct(response_queries.shape, BF16),
-            jax.ShapeDtypeStruct(resp_kv.shape, BF16),
-            jax.ShapeDtypeStruct(prompt_kv.shape, BF16),
+            jax.ShapeDtypeStruct(response_queries.shape, F32),
+            jax.ShapeDtypeStruct(resp_kv.shape, F32),
+            jax.ShapeDtypeStruct((tiles, prompts, ROWS, LANES), BF16),
+            jax.ShapeDtypeStruct((8, LANES), F32),
         ),
         in_specs=[any_space] * 4 + [smem] * 3 + [vmem] * 2,
-        out_specs=(vmem,) * 4,
+        out_specs=(vmem,) * 5,
         scratch_shapes=[
             pltpu.VMEM((prompts, total_len, width), BF16),
             pltpu.VMEM((slots, tokens, qw), BF16),
@@ -329,24 +388,44 @@
             pltpu.VMEM((slots, tokens, qw), BF16),
             pltpu.VMEM((keys, groups * tokens), BF16),
             pltpu.VMEM((keys, groups * tokens), BF16),
-            pltpu.VMEM((slots, tokens, qw), F32),
-            pltpu.VMEM((slots, tokens, width), F32),
-            pltpu.VMEM((np_ * tiles, slots, ROWS, LANES), BF16),
+            pltpu.VMEM((slots, np_ * tiles, ROWS, LANES), BF16),
             pltpu.VMEM((n, slots, ROWS, LANES), BF16),
             pltpu.VMEM((n, info_rows, pl_w), F32),
             pltpu.VMEM((tiles, prompts, ROWS, LANES), BF16),
             pltpu.VMEM((8, pl_w), F32),
             dma((4,)),
-            dma((np_,)), dma((np_,)),
-            dma((n,)), dma((n,)),
+            dma((np_,)), dma((np_,)), dma((np_,)), dma((np_,)),
+            dma((slots, n)), dma((slots, n)),
             dma((n,)), dma((n,)),
             dma((nr,)), dma((nr,)),
         ],
-        compiler_params=pltpu.CompilerParams(collective_id=0, has_side_effects=True),
+        compiler_params=pltpu.CompilerParams(
+            collective_id=0, has_side_effects=True, vmem_limit_bytes=24 * 1024 * 1024
+        ),
     )(
         prompt_kv, response_queries, resp_kv, readout, slot_response, lengths, pair_prompt,
         pair_prompt.reshape(1, pairs), ref_margin.reshape(1, pairs),
     )
+    margins, gq, gkv, gp = pl.pallas_call(
+        finish,
+        name="scale_and_store",
+        out_shape=(
+            jax.ShapeDtypeStruct((1, pairs), F32),
+            jax.ShapeDtypeStruct(response_queries.shape, BF16),
+            jax.ShapeDtypeStruct(resp_kv.shape, BF16),
+            jax.ShapeDtypeStruct(prompt_kv.shape, BF16),
+        ),
+        in_specs=[vmem] * 5,
+        out_specs=(any_space,) * 4,
+        scratch_shapes=[
+            pltpu.VMEM((1, pairs), F32),
+            pltpu.VMEM((slots, tokens, qw), BF16),
+            pltpu.VMEM((slots, tokens, width), BF16),
+            pltpu.VMEM(prompt_kv.shape, BF16),
+            dma((3 * slots + 2,)),
+        ],
+        compiler_params=pltpu.CompilerParams(vmem_limit_bytes=16 * 1024 * 1024),
+    )(*partial_outs)
     return margins.reshape(pairs), gq, gkv, gp
 
 

time: 40.1 us -> 40.6 us (1.012)
  local copies, waits for them, and re-layouts: 4.84 us -> 6.76 us
  Pallas kernels: 34 us -> 32.9 us
    pallas_call x1, Pallas kernels: 34 us -> 31.7 us  [on_device(): pl.pallas_call(functools.partial(kernel, np_, nr), name='dpo_attention',...]
    unnamed x10 -> x16, local copies, waits for them, and re-layouts: 4.84 us -> 6.76 us
    pallas_call x0 -> x1, Pallas kernels: none -> 1.18 us  [on_device(): pl.pallas_call(finish, name='scale_and_store', out_shape=(jax.ShapeDtypeS...]
where the time goes in v2:
time: 40.6 us; the launch traced here: 40.3 us
  Pallas kernels  32.9 us (81%)
  local copies, waits for them, and re-layouts  6.76 us (17%)
  between operations  0.66 us (2%)
    pallas_call x1, Pallas kernels, on_device(): pl.pallas_call(functools.partial(kernel, np_, nr), name='dpo_attention',...  31.7 us
    unnamed x16, local copies, waits for them, and re-layouts  6.76 us
    pallas_call x1, Pallas kernels, on_device(): pl.pallas_call(finish, name='scale_and_store', out_shape=(jax.ShapeDtypeS...  1.18 us

profile of v2, /device:TPU:0, one launch (start us, length us, event | category | flops | bytes accessed | tf_op | source)
XLA Modules:
  0.0 40.3 jit_solution(11435964058497331253)
XLA Ops:
  0.6 0.0 copy-start
  0.6 1.2 %copy-done = bf16[2,128,1792]{2,1,0:T(8,128)(2,1)S(1)} copy-done((bf16[2,128,1792]{2,1,0:T(8,128)(2,1)S(1)}, bf16[2,128,1792]{2,1,0:T(8,128)(2,1)}, u32[]{:S(2)}) %copy-start) | copy-done | bytes 917528
  1.8 0.0 copy-start.1
  1.8 1.2 %copy-done.1 = bf16[2,128,1792]{2,1,0:T(8,128)(2,1)S(1)} copy-done((bf16[2,128,1792]{2,1,0:T(8,128)(2,1)S(1)}, bf16[2,128,1792]{2,1,0:T(8,128)(2,1)}, u32[]{:S(2)}) %copy-start.1) | copy-done | bytes 917528
  3.0 0.0 copy-start.2
  3.0 0.9 %copy-done.2 = bf16[2,128,512]{2,1,0:T(8,128)(2,1)S(1)} copy-done((bf16[2,128,512]{2,1,0:T(8,128)(2,1)S(1)}, bf16[2,128,512]{2,1,0:T(8,128)(2,1)}, u32[]{:S(2)}) %copy-start.2) | copy-done | bytes 262168
  3.9 0.0 copy-start.3
  3.9 0.8 %copy-done.3 = bf16[2,32,512]{2,1,0:T(8,128)(2,1)S(1)} copy-done((bf16[2,32,512]{2,1,0:T(8,128)(2,1)S(1)}, bf16[2,32,512]{2,1,0:T(8,128)(2,1)}, u32[]{:S(2)}) %copy-start.3) | copy-done | bytes 65560
  4.8 0.0 copy-start.4
  4.8 0.7 %copy-done.4 = s32[32]{0:T(128)S(1)} copy-done((s32[32]{0:T(128)S(1)}, s32[32]{0:T(128)}, u32[]{:S(2)}) %copy-start.4) | copy-done | bytes 152
  5.4 0.0 copy-start.5
  5.4 0.7 %copy-done.5 = s32[2]{0:T(128)S(1)} copy-done((s32[2]{0:T(128)S(1)}, s32[2]{0:T(128)}, u32[]{:S(2)}) %copy-start.5) | copy-done | bytes 32
  6.1 0.0 copy-start.6
  6.1 0.7 %copy-done.6 = s32[64]{0:T(128)S(1)} copy-done((s32[64]{0:T(128)S(1)}, s32[64]{0:T(128)}, u32[]{:S(2)}) %copy-start.6) | copy-done | bytes 280
  6.8 0.0 copy-start.7
  6.8 0.7 %copy-done.7 = f32[32]{0:T(128)S(1)} copy-done((f32[32]{0:T(128)S(1)}, f32[32]{0:T(128)}, u32[]{:S(2)}) %copy-start.7) | copy-done | bytes 152
  7.4 31.7 %dpo_attention.1 = (f32[1,32]{1,0:T(1,128)S(1)}, f32[2,128,1792]{2,1,0:T(8,128)S(1)}, f32[2,128,512]{2,1,0:T(8,128)S(1)}, bf16[8,2,16,128]{3,2,1,0:T(8,128)(2,1)S(1)}, f32[8,128]{1,0:T(8,128)S(1)}) custom-call(bf16[2,32,512]{2,1,0:T(8,128)(2,1)S(1)} %copy-done.3, bf16[2,128,1792]{2,1,0:T(8,128)(2,1)S(1)} %copy-done, bf16[2,128,512]{2,1,0:T(8,128)(2,1)S(1)} %copy-done.2, ...), custom_call_target="tpu_custom_call" | custom-call | tf_op jit(solution)/shard_map/dpo_attention/pallas_call | solution.py:372
  39.1 1.2 %scale_and_store.1 = (f32[1,32]{1,0:T(1,128)}, bf16[2,128,1792]{2,1,0:T(8,128)(2,1)}, bf16[2,128,512]{2,1,0:T(8,128)(2,1)}, bf16[2,32,512]{2,1,0:T(8,128)(2,1)}) custom-call(f32[1,32]{1,0:T(1,128)S(1)} %get-tuple-element.13.margins_ref, f32[2,128,1792]{2,1,0:T(8,128)S(1)} %get-tuple-element.14.gq_ref, f32[2,128,512]{2,1,0:T(8,128)S(1)} %get-tuple-element.15.gkv_ref, ...), custom_call_target="tpu_custom_call" | custom-call | tf_op jit(solution)/shard_map/scale_and_store/pallas_call | solution.py:409
Async XLA Ops:
  0.6 1.2 %copy-start = (bf16[2,128,1792]{2,1,0:T(8,128)(2,1)S(1)}, bf16[2,128,1792]{2,1,0:T(8,128)(2,1)}, u32[]{:S(2)}) copy-start(bf16[2,128,1792]{2,1,0:T(8,128)(2,1)} %q_hbm.1) | copy-start | bytes 2752516
  1.8 1.2 %copy-start.1 = (bf16[2,128,1792]{2,1,0:T(8,128)(2,1)S(1)}, bf16[2,128,1792]{2,1,0:T(8,128)(2,1)}, u32[]{:S(2)}) copy-start(bf16[2,128,1792]{2,1,0:T(8,128)(2,1)} %ro_hbm.1) | copy-start | bytes 2752516
  3.0 0.9 %copy-start.2 = (bf16[2,128,512]{2,1,0:T(8,128)(2,1)S(1)}, bf16[2,128,512]{2,1,0:T(8,128)(2,1)}, u32[]{:S(2)}) copy-start(bf16[2,128,512]{2,1,0:T(8,128)(2,1)} %kv_hbm.1) | copy-start | bytes 786436
  3.9 0.8 %copy-start.3 = (bf16[2,32,512]{2,1,0:T(8,128)(2,1)S(1)}, bf16[2,32,512]{2,1,0:T(8,128)(2,1)}, u32[]{:S(2)}) copy-start(bf16[2,32,512]{2,1,0:T(8,128)(2,1)} %prompt_hbm.1) | copy-start | bytes 196612
  4.8 0.7 %copy-start.4 = (s32[32]{0:T(128)S(1)}, s32[32]{0:T(128)}, u32[]{:S(2)}) copy-start(s32[32]{0:T(128)} %pp_ref.1) | copy-start | bytes 388
  5.4 0.7 %copy-start.5 = (s32[2]{0:T(128)S(1)}, s32[2]{0:T(128)}, u32[]{:S(2)}) copy-start(s32[2]{0:T(128)} %slot_ref.1) | copy-start | bytes 28
  6.1 0.7 %copy-start.6 = (s32[64]{0:T(128)S(1)}, s32[64]{0:T(128)}, u32[]{:S(2)}) copy-start(s32[64]{0:T(128)} %len_ref.1) | copy-start | bytes 772
  6.8 0.7 %copy-start.7 = (f32[32]{0:T(128)S(1)}, f32[32]{0:T(128)}, u32[]{:S(2)}) copy-start(f32[32]{0:T(128)} %param.15) | copy-start | bytes 388

commit v3 on v2

--- a/solution.py
+++ b/solution.py
@@ -30,15 +30,15 @@
 
 def kernel(
     np_, nr,
-    prompt_hbm, q_hbm, kv_hbm, ro_hbm, slot_ref, len_ref, pp_ref, ppv_ref, rm_ref,
+    prompt_hbm, q_hbm, kv_hbm, ro_hbm, slot_hbm, len_hbm, pp_hbm, ppv_hbm, rm_hbm,
     margins_out, gq_s, gkv_s, fin_out, coef_out,
-    full, qv, kvv, rov, ds_s, p_s, g_send, g_all, info_all, fin_all, lanes_s,
+    full, qv, kvv, rov, slot_ref, len_ref, pp_ref, ppv_ref, rm_ref, ds_s, p_s, g_send, g_all, info_all, fin_all, lanes_s,
     in_sem, pk_ssem, pk_rsem, pd_ssem, pd_rsem, g_ssem, g_rsem, i_ssem, i_rsem, f_ssem, f_rsem,
 ):
     n = np_ * nr
     prompts, local, width = prompt_hbm.shape
     slots, tokens, _ = q_hbm.shape
-    pairs = rm_ref.shape[1]
+    pairs = rm_hbm.shape[1]
     pl_w = info_all.shape[2]
     groups = QUERY_HEADS // KEY_VALUE_HEADS
     col_tiles = width // LANES
@@ -59,6 +59,11 @@
         pltpu.make_async_copy(q_hbm, qv, in_sem.at[1]),
         pltpu.make_async_copy(kv_hbm, kvv, in_sem.at[2]),
         pltpu.make_async_copy(ro_hbm, rov, in_sem.at[3]),
+        pltpu.make_async_copy(slot_hbm, slot_ref, in_sem.at[4]),
+        pltpu.make_async_copy(len_hbm, len_ref, in_sem.at[5]),
+        pltpu.make_async_copy(pp_hbm, pp_ref, in_sem.at[6]),
+        pltpu.make_async_copy(ppv_hbm, ppv_ref, in_sem.at[7]),
+        pltpu.make_async_copy(rm_hbm, rm_ref, in_sem.at[8]),
     ]
     for c in loads:
         c.start()
@@ -73,8 +78,6 @@
     lax.fori_loop(1, n, greet, 0)
 
     lanes_s[...] = jnp.zeros_like(lanes_s)
-    lanes_s[0:1, 0:pairs] = rm_ref[...]
-    lanes_s[1:2, 0:pairs] = ppv_ref[...].astype(F32)
     info_all[me] = jnp.zeros((info_all.shape[1], pl_w), F32)
 
     loads[0].wait()
@@ -107,6 +110,8 @@
         prompt_copy(p, o).start()
     for c in loads[1:]:
         c.wait()
+    lanes_s[0:1, 0:pairs] = rm_ref[...]
+    lanes_s[1:2, 0:pairs] = ppv_ref[...].astype(F32)
     for o in others:
         prompt_copy(o, p).wait_recv()
         pass_copy(o, half).start()
@@ -176,7 +181,7 @@
             for j in range(groups):
                 h = g * groups + j
                 hc = slice(h * HEAD_SIZE, (h + 1) * HEAD_SIZE)
-                gq_s[s, :, hc] = gqt[:, j * tokens:(j + 1) * tokens].T
+                gq_s[s, :, hc] = gqt[:, j * tokens:(j + 1) * tokens].T.astype(BF16)
             heads = range(g * groups, (g + 1) * groups)
             qs = jnp.concatenate([qv[s, :, h * HEAD_SIZE:(h + 1) * HEAD_SIZE] for h in heads], axis=0)
             rs = jnp.concatenate([rov[s, :, h * HEAD_SIZE:(h + 1) * HEAD_SIZE] for h in heads], axis=0)
@@ -337,7 +342,7 @@
         coef = coef_ref[s:s + 1, 0:1]
         for t in range(pieces):
             rows = slice(t * step, (t + 1) * step)
-            qv[s, rows] = (gq_ref[s, rows] * (coef * scale)).astype(BF16)
+            qv[s, rows] = (gq_ref[s, rows].astype(F32) * (coef * scale)).astype(BF16)
             put(qv.at[s, rows], gq_out.at[s, rows])
         kvv[s] = (gkv_ref[s] * coef).astype(BF16)
         put(kvv.at[s], gkv_out.at[s])
@@ -365,27 +370,31 @@
     info_rows = 2 * slots
     assert nr % 2 == 0
     keys = total_len + tokens
-    any_space = pl.BlockSpec(memory_space=pl.ANY)
+    hbm = pl.BlockSpec(memory_space=pltpu.HBM)
     vmem = pl.BlockSpec(memory_space=pltpu.VMEM)
-    smem = pl.BlockSpec(memory_space=pltpu.SMEM)
     dma = pltpu.SemaphoreType.DMA
     partial_outs = pl.pallas_call(
         functools.partial(kernel, np_, nr),
         name="dpo_attention",
         out_shape=(
             jax.ShapeDtypeStruct((1, pairs), F32),
-            jax.ShapeDtypeStruct(response_queries.shape, F32),
+            jax.ShapeDtypeStruct(response_queries.shape, BF16),
             jax.ShapeDtypeStruct(resp_kv.shape, F32),
             jax.ShapeDtypeStruct((tiles, prompts, ROWS, LANES), BF16),
             jax.ShapeDtypeStruct((8, LANES), F32),
         ),
-        in_specs=[any_space] * 4 + [smem] * 3 + [vmem] * 2,
+        in_specs=[hbm] * 9,
         out_specs=(vmem,) * 5,
         scratch_shapes=[
             pltpu.VMEM((prompts, total_len, width), BF16),
             pltpu.VMEM((slots, tokens, qw), BF16),
             pltpu.VMEM((slots, tokens, width), BF16),
             pltpu.VMEM((slots, tokens, qw), BF16),
+            pltpu.SMEM(slot_response.shape, jnp.int32),
+            pltpu.SMEM(lengths.shape, jnp.int32),
+            pltpu.SMEM(pair_prompt.shape, jnp.int32),
+            pltpu.VMEM((1, pairs), jnp.int32),
+            pltpu.VMEM((1, pairs), F32),
             pltpu.VMEM((keys, groups * tokens), BF16),
             pltpu.VMEM((keys, groups * tokens), BF16),
             pltpu.VMEM((slots, np_ * tiles, ROWS, LANES), BF16),
@@ -393,14 +402,14 @@
             pltpu.VMEM((n, info_rows, pl_w), F32),
             pltpu.VMEM((tiles, prompts, ROWS, LANES), BF16),
             pltpu.VMEM((8, pl_w), F32),
-            dma((4,)),
+            dma((9,)),
             dma((np_,)), dma((np_,)), dma((np_,)), dma((np_,)),
             dma((slots, n)), dma((slots, n)),
             dma((n,)), dma((n,)),
             dma((nr,)), dma((nr,)),
         ],
         compiler_params=pltpu.CompilerParams(
-            collective_id=0, has_side_effects=True, vmem_limit_bytes=24 * 1024 * 1024
+            collective_id=0, has_side_effects=True
         ),
     )(
         prompt_kv, response_queries, resp_kv, readout, slot_response, lengths, pair_prompt,
@@ -416,7 +425,7 @@
             jax.ShapeDtypeStruct(prompt_kv.shape, BF16),
         ),
         in_specs=[vmem] * 5,
-        out_specs=(any_space,) * 4,
+        out_specs=(hbm,) * 4,
         scratch_shapes=[
             pltpu.VMEM((1, pairs), F32),
             pltpu.VMEM((slots, tokens, qw), BF16),
@@ -424,7 +433,6 @@
             pltpu.VMEM(prompt_kv.shape, BF16),
             dma((3 * slots + 2,)),
         ],
-        compiler_params=pltpu.CompilerParams(vmem_limit_bytes=16 * 1024 * 1024),
     )(*partial_outs)
     return margins.reshape(pairs), gq, gkv, gp
 

time: 40.6 us -> 35.1 us (0.86)
  local copies, waits for them, and re-layouts: 6.76 us -> 0 us
  Pallas kernels: 32.9 us -> 34.3 us
    unnamed x16 -> x0, local copies, waits for them, and re-layouts: 6.76 us -> none
    pallas_call x1, Pallas kernels: 1.18 us -> 2.52 us  [on_device(): pl.pallas_call(finish, name='scale_and_store', out_shape=(jax.ShapeDtypeS...]
where the time goes in v3:
time: 35.1 us; the launch traced here: 35 us
  Pallas kernels  34.3 us (98%)
  between operations  0.64 us (2%)
    pallas_call x1, Pallas kernels, on_device(): pl.pallas_call(functools.partial(kernel, np_, nr), name='dpo_attention',...  31.8 us
    pallas_call x1, Pallas kernels, on_device(): pl.pallas_call(finish, name='scale_and_store', out_shape=(jax.ShapeDtypeS...  2.52 us

profile of v3, /device:TPU:0, one launch (start us, length us, event | category | flops | bytes accessed | tf_op | source)
XLA Modules:
  0.0 35.0 jit_solution(17956622065304921096)
XLA Ops:
  0.6 31.8 %dpo_attention.1 = (f32[1,32]{1,0:T(1,128)}, bf16[2,128,1792]{2,1,0:T(8,128)(2,1)}, f32[2,128,512]{2,1,0:T(8,128)}, bf16[8,2,16,128]{3,2,1,0:T(8,128)(2,1)}, f32[8,128]{1,0:T(8,128)}) custom-call(bf16[2,32,512]{2,1,0:T(8,128)(2,1)} %prompt_hbm.1, bf16[2,128,1792]{2,1,0:T(8,128)(2,1)} %q_hbm.1, bf16[2,128,512]{2,1,0:T(8,128)(2,1)} %kv_hbm.1, ...), custom_call_target="tpu_custom_call" | custom-call | tf_op jit(solution)/shard_map/dpo_attention/pallas_call | solution.py:376
  32.4 2.5 %scale_and_store.1 = (f32[1,32]{1,0:T(1,128)}, bf16[2,128,1792]{2,1,0:T(8,128)(2,1)}, bf16[2,128,512]{2,1,0:T(8,128)(2,1)}, bf16[2,32,512]{2,1,0:T(8,128)(2,1)}) custom-call(f32[1,32]{1,0:T(1,128)} %get-tuple-element.13.margins_ref, bf16[2,128,1792]{2,1,0:T(8,128)(2,1)} %get-tuple-element.14.gq_ref, f32[2,128,512]{2,1,0:T(8,128)} %get-tuple-element.15.gkv_ref, ...), custom_call_target="tpu_custom_call" | custom-call | tf_op jit(solution)/shard_map/scale_and_store/pallas_call | solution.py:418
